TPU v7x, 32 devices: a whole 2x2x4 slice. The times are simulated.
32 devices in a mesh: owner: 4 (over x, core), rows: 8 (over z, y).
Axes of the slice: x: 2, y: 2, z: 4, core: 2. Of those that a mesh axis runs over, the one named last changes fastest.
Arguments:
- train_gate: float32 [128, 2048, 768], P('owner', 'rows'), may hold values from -0.1875 to 0.1875
- train_up: float32 [128, 2048, 768], P('owner', 'rows'), may hold values from -0.1875 to 0.1875
- router_weight: float32 [2048, 128], P('rows', 'owner'), may hold values from -0.125 to 0.125
- router_gain: float32 [2048], P('rows'), may hold values from 0.25 to 1.75
Outputs:
- ready_gate: bfloat16 [128, 2048, 768], P(('owner', 'rows'))
- ready_up: bfloat16 [128, 2048, 768], P(('owner', 'rows'))
- scale_gate: float32 [128, 768], P(('owner', 'rows'))
- scale_up: float32 [128, 768], P(('owner', 'rows'))
- serve_router: bfloat16 [2048, 128], replicated
All inputs are finite; a program needn't handle non-finite values.
Results may differ from a plain program's by a relative error of at most 0.001.
Values may be sent and summed in bfloat16 or wider, within the bound.
A program may use at most 192 MiB of HBM per device.

v0:
```python
import jax
import jax.numpy as jnp
from jax import lax
from jax.sharding import PartitionSpec as P


def on_device(train_gate, train_up, router_weight, router_gain):
    total_gate, total_up = lax.psum(
        (jnp.sum(train_gate * train_gate, axis=1), jnp.sum(train_up * train_up, axis=1)), "rows"
    )
    scale_gate = jnp.sqrt(total_gate)
    scale_up = jnp.sqrt(total_up)
    narrow_gate, narrow_up = (
        (train_gate / jnp.expand_dims(scale_gate, 1)).astype(jnp.bfloat16),
        (train_up / jnp.expand_dims(scale_up, 1)).astype(jnp.bfloat16),
    )
    ready_gate, ready_up = (
        lax.all_to_all(narrow_gate, "rows", split_axis=0, concat_axis=1, tiled=True),
        lax.all_to_all(narrow_up, "rows", split_axis=0, concat_axis=1, tiled=True),
    )
    scale_gate = lax.dynamic_slice_in_dim(
        scale_gate, lax.axis_index("rows") * ready_gate.shape[0], ready_gate.shape[0], axis=0
    )
    scale_up = lax.dynamic_slice_in_dim(
        scale_up, lax.axis_index("rows") * ready_up.shape[0], ready_up.shape[0], axis=0
    )
    part_router = (router_weight * router_gain[:, None]).astype(jnp.bfloat16)
    row_router = lax.all_gather(part_router, "rows", axis=0, tiled=True)
    serve_router = lax.all_gather(row_router, "owner", axis=1, tiled=True)
    return (ready_gate, ready_up, scale_gate, scale_up, serve_router)


def solution(mesh):
    return jax.shard_map(
        on_device,
        mesh=mesh,
        in_specs=(
            P("owner", "rows", None),
            P("owner", "rows", None),
            P("rows", "owner"),
            P("rows"),
        ),
        out_specs=(
            P(("owner", "rows"), None, None),
            P(("owner", "rows"), None, None),
            P(("owner", "rows"), None),
            P(("owner", "rows"), None),
            P(),
        ),
        check_vma=False,
    )
```

profile of v0, /device:TPU:0, one launch (start us, length us, event | category | flops | bytes accessed | tf_op | source)
XLA Modules:
  0.0 723.9 jit_solution(15116092223100259474)
XLA Ops:
  7.2 0.0 all-reduce.3.cloned.1.call-start
  7.2 17.3 %multiply_reduce_fusion = (f32[32,768]{1,0:T(8,128)}, f32[32,768]{1,0:T(8,128)}) fusion(f32[32,256,768]{2,1,0:T(8,128)} %param.5, f32[32,256,768]{2,1,0:T(8,128)} %param.4), kind=kLoop, calls=%fused_computation.1 | loop fusion | flops 25116672 | bytes 50528256 | tf_op jit(solution)/shard_map/reduce_sum | solution.py:9
  24.5 0.0 all-reduce.3.cloned.1.call-update
  24.5 73.8 %all-reduce.3.cloned.1.call-done = (f32[32,768]{1,0:T(8,128)}, f32[32,768]{1,0:T(8,128)}) async-done(((f32[32,768]{1,0:T(8,128)}, f32[32,768]{1,0:T(8,128)}), (f32[32,768]{1,0:T(8,128)}, f32[32,768]{1,0:T(8,128)})) %all-reduce.3.cloned.1.call-update) | async-done | bytes 196624 | tf_op jit(solution)/shard_map/psum | solution.py:8
  98.2 0.9 sqrt.6
  99.2 0.0 copy-start
  99.2 13.7 %divide_convert_fusion.1 = bf16[32,256,768]{2,1,0:T(8,128)(2,1)} fusion(f32[32,256,768]{2,1,0:T(8,128)} %param.4, f32[32,768]{1,0:T(8,128)S(1)} %sqrt.6), kind=kLoop, calls=%fused_computation.2 | loop fusion | flops 12582912 | bytes 37847040 | tf_op jit(solution)/shard_map/convert_element_type | solution.py:14
  112.9 5.4 all-to-all-start
  118.2 0.0 copy-done
  118.3 0.0 copy-start.1
  118.3 0.0 copy-start.2
  118.3 13.8 %divide_convert_fusion = bf16[32,256,768]{2,1,0:T(8,128)(2,1)} fusion(f32[32,256,768]{2,1,0:T(8,128)} %param.5, f32[32,768]{1,0:T(8,128)S(1)} %sqrt.7), kind=kLoop, calls=%fused_computation | loop fusion | flops 12582912 | bytes 37847040 | tf_op jit(solution)/shard_map/convert_element_type | solution.py:15
  132.1 257.3 %all-to-all-done = bf16[32,256,768]{2,1,0:T(8,128)(2,1)} async-done(((bf16[32,256,768]{2,1,0:T(8,128)(2,1)}), bf16[32,256,768]{2,1,0:T(8,128)(2,1)}, u32[]{:S(2)}, u32[]{:S(2)}) %all-to-all-start) | async-done | bytes 12582944 | tf_op jit(solution)/shard_map/all_to_all | solution.py:18
  389.4 5.4 all-to-all-start.1
  394.8 0.0 copy-done.1
  394.8 0.0 copy-done.2
  394.8 291.6 %all_gather.6 = bf16[2048,32]{0,1:T(8,128)(2,1)S(1)} all-gather(bf16[256,32]{0,1:T(8,128)(2,1)S(1)} %multiply_convert_fusion), channel_id=1, replica_groups=mesh['owner'=4,'rows'=8] {'rows'}, dimensions={0}, use_global_device_ids=true | all-gather | bytes 147456 | tf_op jit(solution)/shard_map/all_gather | solution.py:28
  686.4 7.1 all_gather.7
  693.5 1.0 copy.14
  694.5 0.6 constant_dynamic-slice_fusion
  695.1 0.6 constant_dynamic-slice_fusion.1
  695.7 10.7 %copy.12 = bf16[8,4,256,768]{3,2,0,1:T(8,128)(2,1)} copy(bf16[8,4,256,768]{3,2,1,0:T(8,128)(2,1)} %bitcast) | data formatting | bytes 25165824 | tf_op jit(solution)/shard_map/all_to_all | solution.py:18
  706.4 0.0 all-to-all-done.1
  706.4 10.7 %copy.13 = bf16[8,4,256,768]{3,2,0,1:T(8,128)(2,1)} copy(bf16[8,4,256,768]{3,2,1,0:T(8,128)(2,1)} %bitcast.3) | data formatting | bytes 25165824 | tf_op jit(solution)/shard_map/all_to_all | solution.py:19
  (2 shorter events, 0.0 us)
Async XLA Ops:
  7.2 91.1 %all-reduce.3.cloned.1.call-start = ((), (), s32[]{:S(2)}) async-start(), calls=%async_computation.2 | async-start | bytes 393216 | tf_op jit(solution)/shard_map/psum | solution.py:8
  99.2 19.1 %copy-start = (f32[32,768]{1,0:T(8,128)S(1)}, f32[32,768]{1,0:T(8,128)}, u32[]{:S(2)}) copy-start(f32[32,768]{1,0:T(8,128)} %get-tuple-element.11) | copy-start | bytes 294916
  112.9 276.5 %all-to-all-start = ((bf16[32,256,768]{2,1,0:T(8,128)(2,1)}), bf16[32,256,768]{2,1,0:T(8,128)(2,1)}, u32[]{:S(2)}, u32[]{:S(2)}) async-start(bf16[32,256,768]{2,1,0:T(8,128)(2,1)} %divide_convert_fusion.1), calls=%async_computation | async-start | bytes 25165824 | tf_op jit(solution)/shard_map/all_to_all | solution.py:18
  118.3 276.5 %copy-start.1 = (f32[256,32]{0,1:T(8,128)S(1)}, f32[256,32]{0,1:T(8,128)}, u32[]{:S(2)}) copy-start(f32[256,32]{0,1:T(8,128)} %param.6) | copy-start | bytes 98308
  118.3 276.5 %copy-start.2 = (f32[256]{0:T(256)S(1)}, f32[256]{0:T(256)}, u32[]{:S(2)}) copy-start(f32[256]{0:T(256)} %param.7) | copy-start | bytes 3076
  389.4 317.0 %all-to-all-start.1 = ((bf16[32,256,768]{2,1,0:T(8,128)(2,1)}), bf16[32,256,768]{2,1,0:T(8,128)(2,1)}, u32[]{:S(2)}, u32[]{:S(2)}) async-start(bf16[32,256,768]{2,1,0:T(8,128)(2,1)} %divide_convert_fusion), calls=%async_computation.1 | async-start | bytes 25165824 | tf_op jit(solution)/shard_map/all_to_all | solution.py:19
Sparse Core Ops, SparseCore 0:
  24.6 73.5 all-reduce.2
where the time goes:
time: 724 us
  waiting for transfers between devices  331 us (46%)
  blocking collectives  299 us (41%)
  other arithmetic  44.7 us (6%)
  local copies, waits for them, and re-layouts  24.5 us (3%)
  between operations  14.1 us (2%)
  starting transfers between devices  10.8 us (1%)
    all_gather x1, blocking collectives, on_device(): row_router = lax.all_gather(part_router, 'rows', axis=0, tiled=True)  292 us
    all_to_all x1, waiting for transfers between devices, on_device(): lax.all_to_all(narrow_gate, 'rows', split_axis=0, concat_axis=1, tiled=True)  257 us
    psum x1, waiting for transfers between devices, on_device(): lax.psum((jnp.sum(train_gate * train_gate, axis=1), jnp.sum(train_up * tr...  73.8 us
    reduce_sum x1, other arithmetic, on_device(): jnp.sum(train_up * train_up, axis=1)  17.3 us
  transfers between devices with their start and end apart: 3, of which 2 were waited for; matrix products, arithmetic and copies ran while one was open for 4% of the time, Pallas kernels for 0%

commit v1 on v0

--- a/solution.py
+++ b/solution.py
@@ -15,7 +15,12 @@
         (train_up / jnp.expand_dims(scale_up, 1)).astype(jnp.bfloat16),
     )
     ready_gate, ready_up = (
-        lax.all_to_all(narrow_gate, "rows", split_axis=0, concat_axis=1, tiled=True),
+        jnp.concatenate(
+            lax.all_to_all(
+                jnp.stack(jnp.split(narrow_gate, lax.axis_size("rows"), axis=0)), "rows", 0, 0
+            ),
+            axis=1,
+        ),
         lax.all_to_all(narrow_up, "rows", split_axis=0, concat_axis=1, tiled=True),
     )
     scale_gate = lax.dynamic_slice_in_dim(

time: 724 us -> 731 us (level)
  local copies, waits for them, and re-layouts: 24.5 us -> 34.5 us
    all_to_all x1 -> x0, local copies, waits for them, and re-layouts: 10.7 us -> none  [on_device(): lax.all_to_all(narrow_gate, 'rows', split_axis=0, concat_axis=1, tiled=True)]
    reshape x0 -> x1, local copies, waits for them, and re-layouts: none -> 10.7 us  [on_device(): jnp.concatenate(lax.all_to_all(jnp.stack(jnp.split(narrow_gate, lax.axis_...]
    unnamed x7 -> x14, local copies, waits for them, and re-layouts: 1.02 us -> 9.72 us
where the time goes in v1:
time: 731 us; the launch traced here: 730 us
  waiting for transfers between devices  331 us (45%)
  blocking collectives  299 us (41%)
  other arithmetic  40.7 us (6%)
  local copies, waits for them, and re-layouts  34.5 us (5%)
  between operations  14.1 us (2%)
  starting transfers between devices  10.9 us (1%)
    all_gather x1, blocking collectives, on_device(): row_router = lax.all_gather(part_router, 'rows', axis=0, tiled=True)  292 us
    all_to_all x1, waiting for transfers between devices, on_device(): lax.all_to_all(jnp.stack(jnp.split(narrow_gate, lax.axis_size('rows'), ax...  257 us
    psum x1, waiting for transfers between devices, on_device(): lax.psum((jnp.sum(train_gate * train_gate, axis=1), jnp.sum(train_up * tr...  73.8 us
    reduce_sum x1, other arithmetic, on_device(): jnp.sum(train_up * train_up, axis=1)  17.3 us
  transfers between devices with their start and end apart: 3, of which 2 were waited for; matrix products, arithmetic and copies ran while one was open for 4% of the time, Pallas kernels for 0%

profile of v1, /device:TPU:0, one launch (start us, length us, event | category | flops | bytes accessed | tf_op | source)
XLA Modules:
  0.0 730.0 jit_solution(3985524110714018230)
XLA Ops:
  7.2 0.0 all-reduce.3.cloned.1.call-start
  7.2 17.3 %multiply_reduce_fusion = (f32[32,768]{1,0:T(8,128)}, f32[32,768]{1,0:T(8,128)}) fusion(f32[32,256,768]{2,1,0:T(8,128)} %param.5, f32[32,256,768]{2,1,0:T(8,128)} %param.4), kind=kLoop, calls=%fused_computation.1 | loop fusion | flops 25116672 | bytes 50528256 | tf_op jit(solution)/shard_map/reduce_sum | solution.py:9
  24.5 0.0 all-reduce.3.cloned.1.call-update
  24.5 73.8 %all-reduce.3.cloned.1.call-done = (f32[32,768]{1,0:T(8,128)}, f32[32,768]{1,0:T(8,128)}) async-done(((f32[32,768]{1,0:T(8,128)}, f32[32,768]{1,0:T(8,128)}), (f32[32,768]{1,0:T(8,128)}, f32[32,768]{1,0:T(8,128)})) %all-reduce.3.cloned.1.call-update) | async-done | bytes 196624 | tf_op jit(solution)/shard_map/psum | solution.py:8
  98.2 0.9 sqrt.6
  99.2 9.7 %divide_convert_fusion.1 = bf16[32,256,768]{2,1,0:T(8,128)(2,1)S(1)} fusion(f32[32,256,768]{2,1,0:T(8,128)} %param.4, f32[32,768]{1,0:T(8,128)S(1)} %sqrt.6), kind=kLoop, calls=%fused_computation.2 | loop fusion | flops 12582912 | bytes 37847040 | tf_op jit(solution)/shard_map/convert_element_type | solution.py:14
  108.9 1.2 fusion.7
  110.1 1.2 fusion.6
  111.3 1.2 fusion.5
  112.6 1.2 fusion.4
  113.8 1.2 fusion.3
  115.1 1.2 fusion.2
  116.3 1.2 fusion.1
  117.6 1.2 fusion
  118.8 0.0 copy-start
  118.8 5.5 all-to-all-start
  124.3 0.0 copy-done
  124.4 13.8 %divide_convert_fusion = bf16[32,256,768]{2,1,0:T(8,128)(2,1)} fusion(f32[32,256,768]{2,1,0:T(8,128)} %param.5, f32[32,768]{1,0:T(8,128)S(1)} %sqrt.7), kind=kLoop, calls=%fused_computation | loop fusion | flops 12582912 | bytes 37847040 | tf_op jit(solution)/shard_map/convert_element_type | solution.py:15
  138.2 0.0 copy-start.1
  138.2 0.0 copy-start.2
  138.2 257.3 %all-to-all-done = bf16[8,4,256,768]{3,2,1,0:T(8,128)(2,1)} async-done(((bf16[8,4,256,768]{3,2,1,0:T(8,128)(2,1)}), bf16[8,4,256,768]{3,2,1,0:T(8,128)(2,1)}, u32[]{:S(2)}, u32[]{:S(2)}) %all-to-all-start) | async-done | bytes 12582944 | tf_op jit(solution)/shard_map/all_to_all | solution.py:19
  395.5 5.4 all-to-all-start.1
  400.9 0.0 copy-done.1
  400.9 0.0 copy-done.2
  400.9 291.6 %all_gather.6 = bf16[2048,32]{0,1:T(8,128)(2,1)S(1)} all-gather(bf16[256,32]{0,1:T(8,128)(2,1)S(1)} %multiply_convert_fusion), channel_id=1, replica_groups=mesh['owner'=4,'rows'=8] {'rows'}, dimensions={0}, use_global_device_ids=true | all-gather | bytes 147456 | tf_op jit(solution)/shard_map/all_gather | solution.py:33
  692.5 7.1 all_gather.7
  699.6 1.0 copy.14
  700.6 0.6 constant_dynamic-slice_fusion
  701.2 0.6 constant_dynamic-slice_fusion.1
  701.8 10.7 %copy.12 = bf16[4,8,256,768]{3,2,1,0:T(8,128)(2,1)} copy(bf16[4,8,256,768]{3,2,0,1:T(8,128)(2,1)} %bitcast.8) | data formatting | bytes 25165824 | tf_op jit(solution)/shard_map/reshape | solution.py:18
  712.5 0.0 all-to-all-done.1
  712.5 10.7 %copy.13 = bf16[8,4,256,768]{3,2,0,1:T(8,128)(2,1)} copy(bf16[8,4,256,768]{3,2,1,0:T(8,128)(2,1)} %bitcast.10) | data formatting | bytes 25165824 | tf_op jit(solution)/shard_map/all_to_all | solution.py:24
  (2 shorter events, 0.0 us)
Async XLA Ops:
  7.2 91.1 %all-reduce.3.cloned.1.call-start = ((), (), s32[]{:S(2)}) async-start(), calls=%async_computation.2 | async-start | bytes 393216 | tf_op jit(solution)/shard_map/psum | solution.py:8
  118.8 5.5 copy-start
  118.8 276.7 %all-to-all-start = ((bf16[8,4,256,768]{3,2,1,0:T(8,128)(2,1)}), bf16[8,4,256,768]{3,2,1,0:T(8,128)(2,1)}, u32[]{:S(2)}, u32[]{:S(2)}) async-start(bf16[8,4,256,768]{3,2,1,0:T(8,128)(2,1)} %fusion), calls=%async_computation | async-start | bytes 25165824 | tf_op jit(solution)/shard_map/all_to_all | solution.py:19
  138.2 262.7 %copy-start.1 = (f32[256,32]{0,1:T(8,128)S(1)}, f32[256,32]{0,1:T(8,128)}, u32[]{:S(2)}) copy-start(f32[256,32]{0,1:T(8,128)} %param.6) | copy-start | bytes 98308
  138.2 262.7 %copy-start.2 = (f32[256]{0:T(256)S(1)}, f32[256]{0:T(256)}, u32[]{:S(2)}) copy-start(f32[256]{0:T(256)} %param.7) | copy-start | bytes 3076
  395.5 317.0 %all-to-all-start.1 = ((bf16[32,256,768]{2,1,0:T(8,128)(2,1)}), bf16[32,256,768]{2,1,0:T(8,128)(2,1)}, u32[]{:S(2)}, u32[]{:S(2)}) async-start(bf16[32,256,768]{2,1,0:T(8,128)(2,1)} %divide_convert_fusion), calls=%async_computation.1 | async-start | bytes 25165824 | tf_op jit(solution)/shard_map/all_to_all | solution.py:24
Sparse Core Ops, SparseCore 0:
  24.6 73.5 all-reduce.2
